TPU v7x, 32 devices: a whole 2x2x4 slice. The times are simulated.
32 devices in a mesh: req: 8 (over y, x, core), head: 4 (over z).
Axes of the slice: x: 2, y: 2, z: 4, core: 2. Of those that a mesh axis runs over, the one named last changes fastest.
Arguments:
- queries: bfloat16 [128, 64, 128], P('req', 'head'), may hold values from -6 to 6
- k_codes: bfloat16 [8192, 16, 8, 128], P('req', None, 'head'), may hold values from -6 to 6
- value_quantized_codes: bfloat16 [8192, 16, 8, 128], P('req', None, 'head'), may hold values from -6 to 6
- key_page_scale: float32 [8192, 8], P('req', 'head'), may hold values from 0.5 to 2
- value_page_scale: float32 [8192, 8], P('req', 'head'), may hold values from 4 to 16
- lengths: int32 [128], P('req'), may hold values from 1 to 2032
- page_table: int32 [128, 128], P('req'), may hold values from -1 to 8191, as said below
- out_weight: bfloat16 [8192, 8192], P('head', 'req'), may hold values from -0.0625 to 0.0625
Outputs:
- attn_out: bfloat16 [128, 8192], P(None, ('req', 'head'))
Inputs may be any that keep to these rules, and one draw needn't show every extreme that they name: `page_table`: entries j below ceil(lengths[r] / 16) name pool pages; all such entries of all requests together name every pool page exactly once. Entries beyond are -1.
All inputs are finite; a program needn't handle non-finite values.
Results may differ from a plain program's by a relative error of at most 0.02.
Values may be sent and summed in bfloat16 or wider, within the bound.
A program may use at most 128 MiB of HBM per device.

v0:
```python
import math

import jax
import jax.numpy as jnp
from jax import lax
from jax.sharding import PartitionSpec as P

floor_score = -1e30


def split_product(member_b, data):
    high_part = data.astype(jnp.bfloat16)
    low_part = (data - high_part.astype(jnp.float32)).astype(jnp.bfloat16)
    first = jnp.dot(member_b, high_part, preferred_element_type=jnp.float32)
    return first + jnp.dot(member_b, low_part, preferred_element_type=jnp.float32)


def locate_pages(all_table, all_lengths, offset, pages_here):
    request_count, table_width = all_table.shape
    flat_ids = all_table.reshape(request_count * table_width)
    local_slot = flat_ids - offset
    inside = (flat_ids >= 0) & (local_slot >= 0) & (local_slot < pages_here)
    target = jnp.where(inside, local_slot, pages_here)
    entry_code = jnp.arange(request_count * table_width, dtype=jnp.int32)
    placed = jnp.zeros((pages_here,), jnp.int32).at[target].set(entry_code, mode="drop")
    owners = placed // table_width
    ranks = placed % table_width
    return (owners, ranks, all_lengths[owners])


def on_device(
    queries,
    k_codes,
    value_quantized_codes,
    key_page_scale,
    value_page_scale,
    lengths,
    page_table,
    out_weight,
):
    pages_here, page_size, kv_local, head_size = k_codes.shape
    rows_here = queries.shape[0]
    heads_local = queries.shape[1]
    query_group_count = heads_local // kv_local
    every_query = lax.all_gather(queries, "req", axis=0, tiled=True)
    all_lengths, all_table = (
        lax.all_gather(lengths, "req", axis=0, tiled=True),
        lax.all_gather(page_table, "req", axis=0, tiled=True),
    )
    request_count, table_width = all_table.shape
    offset = lax.axis_index("req") * pages_here
    owners, page_rank, page_length = locate_pages(all_table, all_lengths, offset, pages_here)
    position = page_rank[:, None] * page_size + jnp.arange(page_size, dtype=jnp.int32)[None, :]
    is_live = (position < page_length[:, None])[:, None, None, :]
    page_query = every_query[owners].reshape(pages_here, kv_local, query_group_count, head_size)
    scores = jnp.einsum("pkgd,ptkd->pkgt", page_query, k_codes, preferred_element_type=jnp.float32)
    scores = scores * (key_page_scale[:, :, None, None] / math.sqrt(head_size))
    page_max = jnp.max(jnp.where(is_live, scores, floor_score), axis=-1)
    weights = jnp.where(is_live, jnp.exp(scores - page_max[..., None]), 0.0).astype(jnp.bfloat16)
    page_sum = jnp.sum(weights.astype(jnp.float32), axis=-1).reshape(pages_here, heads_local)
    page_out = jnp.einsum(
        "pkgt,ptkd->pkgd", weights, value_quantized_codes, preferred_element_type=jnp.float32
    )
    page_out = (page_out * value_page_scale[:, :, None, None]).reshape(
        pages_here, heads_local, head_size
    )
    page_max = page_max.reshape(pages_here, heads_local)
    member = owners[:, None] == jnp.arange(request_count, dtype=jnp.int32)[None, :]
    local_peak = jnp.max(jnp.where(member[:, :, None], page_max[:, None, :], floor_score), axis=0)
    member_b = member.astype(jnp.bfloat16).T
    factor = jnp.exp(page_max - local_peak[owners])
    weighted = (page_out * factor[:, :, None]).reshape(pages_here, heads_local * head_size)
    numerator = split_product(member_b, weighted)
    denominator = split_product(member_b, page_sum * factor)
    numerator, denominator = (numerator, denominator)
    sources = lax.axis_size("req")
    numer_in = lax.all_to_all(
        numerator.reshape(sources, rows_here, heads_local * head_size),
        "req",
        split_axis=0,
        concat_axis=0,
        tiled=True,
    )
    denom_in = lax.all_to_all(
        denominator.reshape(sources, rows_here, heads_local),
        "req",
        split_axis=0,
        concat_axis=0,
        tiled=True,
    )
    peak_in = lax.all_to_all(
        local_peak.reshape(sources, rows_here, heads_local),
        "req",
        split_axis=0,
        concat_axis=0,
        tiled=True,
    )
    row_count = numer_in.shape[1]
    overall = jnp.max(peak_in, axis=0)
    factor = jnp.exp(peak_in - overall[None])
    numer_sum = jnp.sum(
        numer_in.reshape(sources, row_count, heads_local, head_size) * factor[..., None], axis=0
    )
    denom_sum = jnp.sum(denom_in * factor, axis=0)
    attention = (numer_sum / denom_sum[..., None]).reshape(row_count, heads_local * head_size)
    attention = attention.astype(jnp.bfloat16)
    terms = jnp.dot(
        lax.all_gather(attention, "req", axis=0, tiled=True),
        out_weight,
        preferred_element_type=jnp.float32,
    )
    return lax.psum_scatter(terms.astype(jnp.bfloat16), "head", scatter_dimension=1, tiled=True)


def solution(mesh):
    in_specs = (
        P("req", "head", None),
        P("req", None, "head", None),
        P("req", None, "head", None),
        P("req", "head"),
        P("req", "head"),
        P("req"),
        P("req", None),
        P("head", "req"),
    )
    out_specs = P(None, ("req", "head"))
    return jax.shard_map(
        on_device, mesh=mesh, in_specs=in_specs, out_specs=out_specs, check_vma=False
    )
```

profile of v0, /device:TPU:0, one launch (start us, length us, event | category | flops | bytes accessed | tf_op | source)
XLA Modules:
  0.0 246.5 jit_solution(17993828565912308326)
XLA Ops:
  6.5 1.2 dynamic-slice
  8.4 0.9 dynamic-update-slice
  9.3 9.5 %all-reduce = s32[128]{0:T(128)S(1)} all-reduce(s32[128]{0:T(128)S(1)} %dynamic-update-slice), channel_id=1, replica_groups=mesh['req'=8,'head'=4] {'req'}, use_global_device_ids=true, to_apply=%add | all-reduce | flops 128 | bytes 1024
  18.8 0.7 broadcast_multiply_fusion.1
  19.5 8.6 %all_gather.12 = s32[128,128]{1,0:T(8,128)S(1)} all-gather(s32[16,128]{1,0:T(8,128)} %param.14), channel_id=1, replica_groups=mesh['req'=8,'head'=4] {'req'}, dimensions={0}, use_global_device_ids=true | all-gather | bytes 73728 | tf_op jit(solution)/shard_map/all_gather | solution.py:48
  28.1 0.2 compare_select_fusion
  28.3 60.3 %scatter_custom_fusion = s32[1024]{0:T(1024)S(1)} fusion(s32[16384]{0:T(1024)S(1)} %bitcast.101, s32[16384]{0:T(1024)S(1)} %iota.18, s32[]{:T(128)} %constant.37.clone.1), kind=kCustom, calls=%fused_computation.56 | custom fusion | bytes 4100 | tf_op jit(solution)/shard_map/scatter | solution.py:25
  88.7 0.2 iota_compare_fusion
  88.9 0.2 copy.55
  89.1 9.5 %all_gather.14 = bf16[128,16,128]{2,1,0:T(8,128)(2,1)S(1)} all-gather(bf16[16,16,128]{2,1,0:T(8,128)(2,1)} %param.8), channel_id=1, replica_groups=mesh['req'=8,'head'=4] {'req'}, dimensions={0}, use_global_device_ids=true | all-gather | bytes 589824 | tf_op jit(solution)/shard_map/all_gather | solution.py:45
  98.6 6.6 %gather_fusion = s32[1024]{0:T(1024)S(1)} fusion(s32[128]{0:T(128)S(1)} %all-reduce, s32[1024]{0:T(1024)S(1)} %get-tuple-element.7), kind=kCustom, calls=%fused_computation | custom fusion | bytes 12288 | tf_op jit(solution)/shard_map/gather | solution.py:28
  105.2 8.5 %gather_fusion.1 = bf16[1024,16,128]{2,1,0:T(8,128)(2,1)} fusion(bf16[128,16,128]{2,1,0:T(8,128)(2,1)S(1)} %all_gather.14, s32[1024]{0:T(1024)S(1)} %get-tuple-element.7), kind=kCustom, calls=%fused_computation.1 | custom fusion | bytes 8392704 | tf_op jit(solution)/shard_map/gather | solution.py:55
  113.7 0.3 add_compare_fusion
  114.0 10.4 %select_reduce_fusion.1 = (f32[1024,2,8]{2,1,0:T(2,128)S(1)}, f32[1024,2,8,16]{3,2,1,0:T(8,128)}) fusion(f32[1024,2]{1,0:T(8,128)S(1)} %copy.55, pred[1024,16]{1,0:T(8,128)(4,1)S(1)} %add_compare_fusion, bf16[1024,16,2,128]{3,2,1,0:T(2,128)(2,1)} %param.9, bf16[1024,16,128]{2,1,0:T(8,128)(2,1)} %gather_fusion.1), kind=kOutput, calls=%fused_computation.13 | convolution fusion | flops 67878912 | bytes 13721600 | tf_op jit(solution)/shard_map/pkgd,ptkd->pkgt/dot_general | solution.py:56
  124.4 0.4 copy.58
  124.8 0.2 copy.59
  125.0 5.2 %select_reduce_fusion = f32[128,16]{0,1:T(8,128)S(1)} fusion(f32[1024,16]{1,0:T(8,128)S(1)} %copy.59, pred[1024,128]{1,0:T(8,128)(4,1)S(1)} %iota_compare_fusion), kind=kLoop, calls=%fused_computation.11 | loop fusion | flops 4192256 | bytes 204800 | tf_op jit(solution)/shard_map/reduce_max | solution.py:69
  130.3 0.1 reshape.149
  130.4 0.7 reshape.194
  131.1 3.5 %all-to-all-start.1 = ((f32[8,1,256]{2,1,0:T(1,128)}), f32[8,1,256]{2,1,0:T(1,128)S(1)}, u32[]{:S(2)}, u32[]{:S(2)}) async-start(f32[8,1,256]{2,1,0:T(1,128)} %reshape.194), calls=%async_computation.1 | async-start | bytes 16384 | tf_op jit(solution)/shard_map/all_to_all | solution.py:91
  134.6 0.1 copy.60
  134.7 1.1 copy.57
  135.8 2.8 %gather_fusion.2 = f32[1024,16]{1,0:T(8,128)S(1)} fusion(f32[128,16]{1,0:T(8,128)S(1)} %copy.60, s32[1024]{0:T(1024)S(1)} %get-tuple-element.7), kind=kCustom, calls=%fused_computation.2 | custom fusion | bytes 135168 | tf_op jit(solution)/shard_map/gather | solution.py:71
  138.6 0.2 copy.61
  138.8 0.2 copy.62
  139.0 9.6 %convert_reduce_fusion = f32[1024,2,8]{2,1,0:T(2,128)S(1)} fusion(f32[1024,2,8]{2,1,0:T(2,128)S(1)} %get-tuple-element.10, f32[1024,2,8,16]{3,2,1,0:T(8,128)} %get-tuple-element.11, f32[1024,2]{1,0:T(8,128)S(1)} %copy.55, pred[1024,16]{1,0:T(8,128)(4,1)S(1)} %add_compare_fusion), kind=kLoop, calls=%fused_computation.9 | loop fusion | flops 1556480 | bytes 1204224 | tf_op jit(solution)/shard_map/reduce_sum | solution.py:60
  148.6 0.4 copy.65
  149.0 0.3 fusion.13
  149.3 11.1 %broadcast_multiply_fusion = f32[1024,2,8,128]{3,2,1,0:T(8,128)S(1)} fusion(f32[1024,2]{1,0:T(8,128)} %copy.57, bf16[1024,16,2,128]{3,2,1,0:T(2,128)(2,1)} %param.10, f32[1024,2,8,16]{3,2,1,0:T(8,128)} %get-tuple-element.11, f32[1024,2,8]{2,1,0:T(2,128)S(1)} %get-tuple-element.10, f32[1024,2]{1,0:T(8,128)S(1)} %copy.55, ...), kind=kOutput, calls=%fused_computation.16 | convolution fusion | flops 70254592 | bytes 17924096 | tf_op jit(solution)/shard_map/pkgt,ptkd->pkgd/dot_general | solution.py:61
  160.5 2.3 mul.61
  162.8 4.8 %fusion.10 = f32[128,2048]{1,0:T(8,128)S(1)} fusion(f32[128,8,16,128]{3,2,1,0:T(8,128)S(1)} %bitcast.92, f32[128,8,16,128]{3,2,1,0:T(8,128)S(1)} %bitcast.94, s32[1024]{0:T(1024)S(1)} %get-tuple-element.8), kind=kOutput, calls=%fused_computation.18 | convolution fusion | flops 541196288 | bytes 17829888 | tf_op jit(solution)/shard_map/dot_general | solution.py:14
  167.6 0.3 convolution_add_fusion
  167.9 0.1 reshape.151
  168.0 0.7 reshape.196
  168.7 4.0 %all-to-all-start.2 = ((f32[8,1,256]{2,1,0:T(1,128)}), f32[8,1,256]{2,1,0:T(1,128)S(1)}, u32[]{:S(2)}, u32[]{:S(2)}) async-start(f32[8,1,256]{2,1,0:T(1,128)} %reshape.196), calls=%async_computation.2 | async-start | bytes 16384 | tf_op jit(solution)/shard_map/all_to_all | solution.py:84
  172.7 14.2 %fusion.12 = f32[128,2048]{1,0:T(8,128)} fusion(f32[128,2048]{1,0:T(8,128)S(1)} %fusion.10, f32[128,8,16,128]{3,2,1,0:T(8,128)} %bitcast.93, f32[128,8,16,128]{3,2,1,0:T(8,128)} %bitcast.95, s32[1024]{0:T(1024)S(1)} %get-tuple-element.8), kind=kOutput, calls=%fused_computation.19 | convolution fusion | flops 547749888 | bytes 18878464 | tf_op jit(solution)/shard_map/dot_general | solution.py:15
  186.8 4.2 %all-to-all-start = ((f32[8,16,2048]{2,1,0:T(8,128)}), f32[8,16,2048]{2,1,0:T(8,128)S(1)}, u32[]{:S(2)}, u32[]{:S(2)}) async-start(f32[8,16,2048]{2,1,0:T(8,128)} %bitcast.5), calls=%async_computation | async-start | bytes 2097152 | tf_op jit(solution)/shard_map/all_to_all | solution.py:77
  191.1 0.5 broadcast.139
  191.6 0.7 reduce.1
  192.3 0.7 reduce.2
  193.3 0.3 mul.64
  193.7 0.2 mul.65
  193.8 12.6 %all-to-all-done = f32[8,16,2048]{2,1,0:T(8,128)S(1)} async-done(((f32[8,16,2048]{2,1,0:T(8,128)}), f32[8,16,2048]{2,1,0:T(8,128)S(1)}, u32[]{:S(2)}, u32[]{:S(2)}) %all-to-all-start) | async-done | bytes 1048608 | tf_op jit(solution)/shard_map/all_to_all | solution.py:77
  206.4 0.1 multiply_reduce_fusion
  206.5 0.1 div.35
  206.7 8.9 %all_gather.15 = bf16[128,2048]{1,0:T(8,128)(2,1)S(1)} all-gather(bf16[16,2048]{1,0:T(8,128)(2,1)S(1)} %fusion.20), channel_id=1, replica_groups=mesh['req'=8,'head'=4] {'req'}, dimensions={0}, use_global_device_ids=true | all-gather | bytes 589824 | tf_op jit(solution)/shard_map/all_gather | solution.py:108
  215.6 3.6 %convolution_convert_fusion = bf16[128,1024]{1,0:T(8,128)(2,1)} fusion(bf16[128,2048]{1,0:T(8,128)(2,1)S(1)} %all_gather.15, bf16[2048,1024]{1,0:T(8,128)(2,1)} %param.15), kind=kOutput, calls=%fused_computation.20 | convolution fusion | flops 537001984 | bytes 4980736 | tf_op jit(solution)/shard_map/dot_general | solution.py:107
  219.2 20.4 %reduce-scatter.2.cloned.1.call-done = bf16[128,256]{1,0:T(8,128)(2,1)} async-done(((bf16[128,1024]{1,0:T(8,128)(2,1)}), bf16[128,256]{1,0:T(8,128)(2,1)}) %reduce-scatter.2.cloned.1.call-update) | async-done | bytes 65552 | tf_op jit(solution)/shard_map/reduce_scatter | solution.py:112
  (25 shorter events, 0.6 us)
Async XLA Ops:
  114.0 20.7 %copy-start.2 = (f32[1024,2]{0,1:T(2,128)S(1)}, f32[1024,2]{0,1:T(2,128)}, u32[]{:S(2)}) copy-start(f32[1024,2]{0,1:T(2,128)} %param.12) | copy-start | bytes 24580
  131.1 37.7 %all-to-all-start.1 = ((f32[8,1,256]{2,1,0:T(1,128)}), f32[8,1,256]{2,1,0:T(1,128)S(1)}, u32[]{:S(2)}, u32[]{:S(2)}) async-start(f32[8,1,256]{2,1,0:T(1,128)} %reshape.194), calls=%async_computation.1 | async-start | bytes 16384 | tf_op jit(solution)/shard_map/all_to_all | solution.py:91
  160.4 7.1 %copy-start.1 = (f32[1024,2,8,128]{3,2,1,0:T(8,128)}, f32[1024,2,8,128]{3,2,1,0:T(8,128)S(1)}, u32[]{:S(2)}) copy-start(f32[1024,2,8,128]{3,2,1,0:T(8,128)S(1)} %broadcast_multiply_fusion) | copy-start | bytes 25165828
  162.8 4.8 %copy-start = (f32[1024,16,128]{2,1,0:T(8,128)}, f32[1024,16,128]{2,1,0:T(8,128)S(1)}, u32[]{:S(2)}) copy-start(f32[1024,16,128]{2,1,0:T(8,128)S(1)} %mul.61) | copy-start | bytes 25165828
  168.7 18.1 %all-to-all-start.2 = ((f32[8,1,256]{2,1,0:T(1,128)}), f32[8,1,256]{2,1,0:T(1,128)S(1)}, u32[]{:S(2)}, u32[]{:S(2)}) async-start(f32[8,1,256]{2,1,0:T(1,128)} %reshape.196), calls=%async_computation.2 | async-start | bytes 16384 | tf_op jit(solution)/shard_map/all_to_all | solution.py:84
  186.8 19.6 %all-to-all-start = ((f32[8,16,2048]{2,1,0:T(8,128)}), f32[8,16,2048]{2,1,0:T(8,128)S(1)}, u32[]{:S(2)}, u32[]{:S(2)}) async-start(f32[8,16,2048]{2,1,0:T(8,128)} %bitcast.5), calls=%async_computation | async-start | bytes 2097152 | tf_op jit(solution)/shard_map/all_to_all | solution.py:77
  191.0 48.7 %reduce-scatter.2.cloned.1.call-start = ((), (), s32[]{:S(2)}) async-start(), calls=%async_computation.4 | async-start | bytes 327680 | tf_op jit(solution)/shard_map/reduce_scatter | solution.py:112
Sparse Core Ops, SparseCore 0:
  219.4 20.2 reduce-scatter.1
where the time goes:
time: 247 us
  local copies, waits for them, and re-layouts  88.4 us (36%)
  matrix products  44.7 us (18%)
  blocking collectives  36.5 us (15%)
  waiting for transfers between devices  33.1 us (13%)
  other arithmetic  17.9 us (7%)
  between operations  14.4 us (6%)
  starting transfers between devices  11.7 us (5%)
    scatter x1, local copies, waits for them, and re-layouts, locate_pages(): jnp.zeros((pages_here,), jnp.int32).at[target].set(entry_code, mode='drop')  60.3 us
    reduce_scatter x1, waiting for transfers between devices, on_device(): lax.psum_scatter(terms.astype(jnp.bfloat16), 'head', scatter_dimension=1,...  20.4 us
    dot_general x2, matrix products, split_product(): jnp.dot(member_b, low_part, preferred_element_type=jnp.float32)  14.5 us
    all_to_all x1, waiting for transfers between devices, on_device(): lax.all_to_all(numerator.reshape(sources, rows_here, heads_local * head_s...  12.6 us
    dot_general x1, matrix products, on_device(): jnp.einsum('pkgt,ptkd->pkgd', weights, value_quantized_codes, preferred_e...  11.1 us
    dot_general x1, matrix products, on_device(): jnp.einsum('pkgd,ptkd->pkgt', page_query, k_codes, preferred_element_type...  10.4 us
    reduce_sum x1, other arithmetic, on_device(): jnp.sum(weights.astype(jnp.float32), axis=-1)  9.62 us
    all_gather x1, blocking collectives, on_device(): every_query = lax.all_gather(queries, 'req', axis=0, tiled=True)  9.51 us
  transfers between devices with their start and end apart: 4, of which 2 were waited for; matrix products, arithmetic and copies ran while one was open for 21% of the time, Pallas kernels for 0%

commit v1 on v0

v1 whole, which is shorter than its diff:
```python
import functools
import math

import jax
import jax.numpy as jnp
from jax import lax
from jax.experimental import pallas as pl
from jax.experimental.pallas import tpu as pltpu
from jax.sharding import PartitionSpec as P

floor_score = -1e30
DIGIT = 32
GROUP = 8
LANES = 128


def locate_kernel(page_size, table_ref, lengths_ref, out_ref, acc):
    requests, width = table_ref.shape
    rows = out_ref.shape[0]
    step = 8
    acc[...] = jnp.zeros_like(acc)
    iota_hi = lax.broadcasted_iota(jnp.int32, (rows, width), 0)
    iota_lo = lax.broadcasted_iota(jnp.int32, (DIGIT, width), 0)
    entry = lax.broadcasted_iota(jnp.int32, (1, width), 1) * page_size

    def body(i, carry):
        lefts, rights = [], []
        block = table_ref[pl.ds(pl.multiple_of(i * step, step), step), :]
        for s in range(step):
            r = i * step + s
            row = block[s : s + 1, :]
            hi = row >> 5
            lo = row & (DIGIT - 1)
            live = jnp.minimum(lengths_ref[r] - entry, page_size).astype(jnp.float32)
            lefts.append(jnp.where(iota_hi == hi, 1.0, 0.0).astype(jnp.bfloat16))
            same = iota_lo == lo
            r_high = (r // 256).astype(jnp.float32)
            r_low = (r % 256).astype(jnp.float32)
            parts = [
                jnp.where(same, r_high, 0.0),
                jnp.where(same, r_low, 0.0),
                jnp.where(same, live, 0.0),
            ]
            rights.append(jnp.concatenate(parts, axis=0).astype(jnp.bfloat16))
        left = jnp.concatenate(lefts, axis=1)
        right = jnp.concatenate(rights, axis=1)
        acc[...] += lax.dot_general(
            left, right, (((1,), (1,)), ((), ())), preferred_element_type=jnp.float32
        )
        return carry

    lax.fori_loop(0, requests // step, body, 0)
    out_ref[...] = acc[...]


def attend_kernel(
    kv_local,
    q_ref,
    member_ref,
    scale_ref,
    bias_ref,
    block_ref,
    vscale_ref,
    k_ref,
    v_ref,
    out_ref,
    q_rows,
    m_rows,
    sums,
    shift,
    extra,
):
    heads, pages, dim = q_rows.shape
    requests = q_ref.shape[0]
    group_rows = block_ref.shape[1]
    per_head = heads // kv_local
    steps = pl.num_programs(0)
    pid = pl.program_id(0)
    groups = k_ref.shape[0] // group_rows

    @pl.when(pid == 0)
    def _():
        member = member_ref[...].astype(jnp.bfloat16)

        def pick(i, carry):
            cols = q_ref[:, pl.ds(pl.multiple_of(i * 2 * dim, 2 * dim), 2 * dim)]
            got = jnp.dot(member, cols, preferred_element_type=jnp.float32)
            q_rows[2 * i] = got[:, :dim]
            q_rows[2 * i + 1] = got[:, dim:]
            return carry

        lax.fori_loop(0, heads // 2, pick, 0)

    def group(i, carry):
        g = pid * groups + i
        p0 = pl.multiple_of(g * GROUP, GROUP)
        q = jnp.concatenate([q_rows[h, pl.ds(p0, GROUP), :] for h in range(heads)], axis=0)
        start = pl.multiple_of(i * group_rows, group_rows)
        kk = k_ref[pl.ds(start, group_rows), :]
        vv = v_ref[pl.ds(start, group_rows), :]
        s = lax.dot_general(
            q.astype(jnp.bfloat16), kk, (((1,), (1,)), ((), ())), preferred_element_type=jnp.float32
        )
        s = (s * scale_ref[pl.ds(g, 1), :] + bias_ref[pl.ds(g, 1), :]) + block_ref[...]
        top = jnp.max(s, axis=1, keepdims=True)
        w = jnp.exp(s - top).astype(jnp.bfloat16)
        both = jnp.concatenate([vv, jnp.ones_like(vv)], axis=1)
        o = jnp.dot(w, both, preferred_element_type=jnp.float32)
        factors = [vscale_ref[pl.ds(p0, GROUP), k : k + 1] for k in range(kv_local)]
        for h in range(heads):
            rows = slice(h * GROUP, (h + 1) * GROUP)
            sums[h, pl.ds(p0, GROUP), :dim] = o[rows, :dim] * factors[h // per_head]
            sums[h, pl.ds(p0, GROUP), dim:] = o[rows, dim:]
            m_rows[h, pl.ds(p0, GROUP), :] = jnp.broadcast_to(top[rows], (GROUP, dim))
        return carry

    lax.fori_loop(0, groups, group, 0, unroll=4)

    @pl.when(pid == steps - 1)
    def _():
        shift[...] = jnp.zeros_like(shift)
        extra[...] = jnp.zeros_like(extra)
        lane = lax.broadcasted_iota(jnp.int32, extra.shape, 1)

        def finish(h, carry):
            inside = member_ref[...] > 0.5
            top = jnp.concatenate([m_rows[h]] * (requests // dim), axis=1)
            peak = jnp.max(jnp.where(inside, top, floor_score), axis=0, keepdims=True)
            peak = peak.astype(jnp.bfloat16).astype(jnp.float32)
            f = jnp.where(inside, jnp.exp(top - peak), 0.0).astype(jnp.bfloat16)
            got = lax.dot_general(
                f,
                sums[h].astype(jnp.bfloat16),
                (((0,), (0,)), ((), ())),
                preferred_element_type=jnp.float32,
            )
            cols = pl.ds(pl.multiple_of(h * dim, dim), dim)
            out_ref[:, cols] = got[:, :dim].astype(jnp.bfloat16)
            den = got[:, dim:]
            den_high = den.astype(jnp.bfloat16).astype(jnp.float32)
            kept = jnp.where(lane == h, den_high, extra[...])
            extra[...] = jnp.where(lane == heads + h, den - den_high, kept)
            shift[pl.ds(2 * heads + h, 1), :] = peak
            return carry

        lax.fori_loop(0, heads, finish, 0)
        tail = jnp.where(lane < 2 * heads, extra[...], shift[...].T)
        out_ref[:, heads * dim :] = tail.astype(jnp.bfloat16)


def on_device(
    queries,
    k_codes,
    value_quantized_codes,
    key_page_scale,
    value_page_scale,
    lengths,
    page_table,
    out_weight,
):
    pages, page_size, kv_local, dim = k_codes.shape
    rows_here, heads, _ = queries.shape
    per_head = heads // kv_local
    width = heads * dim
    vmem = pl.BlockSpec(memory_space=pltpu.VMEM)
    smem = pl.BlockSpec(memory_space=pltpu.SMEM)

    table = lax.all_gather(page_table, "req", axis=0, tiled=True)
    all_lengths = lax.all_gather(lengths, "req", axis=0, tiled=True)
    q_all = lax.all_gather(queries.reshape(rows_here, width), "req", axis=0, tiled=True)
    requests = table.shape[0]
    sources = lax.axis_size("req")
    local_table = table - lax.axis_index("req") * pages

    found = pl.pallas_call(
        functools.partial(locate_kernel, page_size),
        out_shape=jax.ShapeDtypeStruct((pages // DIGIT, 3 * DIGIT), jnp.float32),
        in_specs=[vmem, smem],
        out_specs=vmem,
        scratch_shapes=[pltpu.VMEM((pages // DIGIT, 3 * DIGIT), jnp.float32)],
        name="locate",
    )(local_table, all_lengths)
    owner = (found[:, :DIGIT] * 256.0 + found[:, DIGIT : 2 * DIGIT]).reshape(pages)
    live = found[:, 2 * DIGIT :].reshape(pages)
    ids = jnp.arange(requests, dtype=jnp.int32).astype(jnp.float32)
    member = (owner[:, None] == ids[None, :]).astype(jnp.float32)

    page_rows = page_size * kv_local
    group_rows = GROUP * page_rows
    token = jnp.arange(page_size, dtype=jnp.int32).astype(jnp.float32)[None, :, None]
    full = (pages, page_size, kv_local)
    bias = jnp.where(jnp.broadcast_to(token < live[:, None, None], full), 0.0, floor_score)
    bias = bias.reshape(pages // GROUP, group_rows)
    scale = jnp.broadcast_to(key_page_scale[:, None, :] / math.sqrt(dim), full)
    scale = scale.reshape(pages // GROUP, group_rows)
    row = jnp.arange(heads * GROUP, dtype=jnp.int32)[:, None]
    col = jnp.arange(group_rows, dtype=jnp.int32)[None, :]
    same = (row % GROUP == col // page_rows) & (row // GROUP // per_head == col % kv_local)
    block = jnp.where(same, 0.0, floor_score).astype(jnp.float32)

    k_rows = k_codes.reshape(pages * page_rows, dim)
    v_rows = value_quantized_codes.reshape(pages * page_rows, dim)
    block_pages = 128
    steps = pages // block_pages
    whole = lambda shape: pl.BlockSpec(shape, lambda i: (0,) * len(shape))
    stream = pl.BlockSpec((block_pages * page_rows, dim), lambda i: (i, 0))
    partial_sums = pl.pallas_call(
        functools.partial(attend_kernel, kv_local),
        grid=(steps,),
        out_shape=jax.ShapeDtypeStruct((requests, width + LANES), jnp.bfloat16),
        in_specs=[vmem, vmem, vmem, vmem, vmem, vmem, stream, stream],
        out_specs=whole((requests, width + LANES)),
        scratch_shapes=[
            pltpu.VMEM((heads, pages, dim), jnp.float32),
            pltpu.VMEM((heads, pages, dim), jnp.float32),
            pltpu.VMEM((heads, pages, 2 * dim), jnp.float32),
            pltpu.VMEM((LANES, requests), jnp.float32),
            pltpu.VMEM((requests, LANES), jnp.float32),
        ],
        compiler_params=pltpu.CompilerParams(
            vmem_limit_bytes=60 * 1024 * 1024, dimension_semantics=("arbitrary",)
        ),
        name="attend",
    )(q_all, member, scale, bias, block, value_page_scale, k_rows, v_rows)

    got = lax.all_to_all(
        partial_sums.reshape(sources, rows_here, width + LANES),
        "req",
        split_axis=0,
        concat_axis=0,
        tiled=True,
    ).astype(jnp.float32)
    tail = got[:, :, width:]
    den = tail[:, :, :heads] + tail[:, :, heads : 2 * heads]
    peak = tail[:, :, 2 * heads : 3 * heads]
    factor = jnp.exp(peak - jnp.max(peak, axis=0)[None])
    factor = factor / jnp.sum(den * factor, axis=0)[None]
    numer = got[:, :, :width].reshape(sources, rows_here, heads, dim)
    attention = jnp.sum(numer * factor[..., None], axis=0).reshape(rows_here, width)
    terms = jnp.dot(
        lax.all_gather(attention.astype(jnp.bfloat16), "req", axis=0, tiled=True),
        out_weight,
        preferred_element_type=jnp.float32,
    )
    return lax.psum_scatter(terms.astype(jnp.bfloat16), "head", scatter_dimension=1, tiled=True)


def solution(mesh):
    in_specs = (
        P("req", "head", None),
        P("req", None, "head", None),
        P("req", None, "head", None),
        P("req", "head"),
        P("req", "head"),
        P("req"),
        P("req", None),
        P("head", "req"),
    )
    out_specs = P(None, ("req", "head"))
    return jax.shard_map(
        on_device, mesh=mesh, in_specs=in_specs, out_specs=out_specs, check_vma=False
    )
```

time: 247 us -> 157 us (0.64)
  local copies, waits for them, and re-layouts: 88.4 us -> 28.6 us
  matrix products: 44.7 us -> 3.64 us
  Pallas kernels: 0 us -> 34.4 us
  blocking collectives: 36.5 us -> 51.5 us
  other arithmetic: 17.9 us -> 3.99 us
  waiting for transfers between devices: 33.1 us -> 20.4 us
  starting transfers between devices: 11.7 us -> 0.01 us
    scatter x1 -> x0, local copies, waits for them, and re-layouts: 60.3 us -> none  [locate_pages(): jnp.zeros((pages_here,), jnp.int32).at[target].set(entry_code, mode='drop')]
    dot_general x7 -> x1, matrix products: 44.7 us -> 3.64 us  [on_device(): jnp.dot(lax.all_gather(attention.astype(jnp.bfloat16), 'req', axis=0, til...]
    pallas_call x0 -> x2, Pallas kernels: none -> 34.4 us  [the longest x1 29.9 us: on_device(): pl.pallas_call(functools.partial(attend_kernel, kv_local), grid=(steps,),...]
    gather x4 -> x0, local copies, waits for them, and re-layouts: 18 us -> none  [the longest x1 8.48 us: on_device(): every_query[owners]]
    reshape x5 -> x2, local copies, waits for them, and re-layouts: 0.4 us -> 14.9 us  [the longest x1 7.48 us: on_device(): scale = scale.reshape(pages // GROUP, group_rows)]
    all_to_all x0 -> x1, blocking collectives: none -> 13.5 us  [on_device(): lax.all_to_all(partial_sums.reshape(sources, rows_here, width + LANES), '...]
    all_to_all x3 -> x0, waiting for transfers between devices: 12.6 us -> none  [the longest x1 12.6 us: on_device(): lax.all_to_all(numerator.reshape(sources, rows_here, heads_local * head_s...]
    all_to_all x3 -> x0, starting transfers between devices: 11.7 us -> none  [the longest x1 4.2 us: on_device(): lax.all_to_all(numerator.reshape(sources, rows_here, heads_local * head_s...]
  transfers between devices with their start and end apart: 4 -> 1, of which waited for: 2 -> 1; matrix products, arithmetic and copies ran while one was open for 21% -> 0% of each run, Pallas kernels for 0% -> 0%
where the time goes in v1:
time: 157 us
  blocking collectives  51.5 us (33%)
  Pallas kernels  34.4 us (22%)
  local copies, waits for them, and re-layouts  28.6 us (18%)
  waiting for transfers between devices  20.4 us (13%)
  between operations  14.2 us (9%)
  other arithmetic  3.99 us (3%)
  matrix products  3.64 us (2%)
    pallas_call x1, Pallas kernels, on_device(): pl.pallas_call(functools.partial(attend_kernel, kv_local), grid=(steps,),...  29.9 us
    reduce_scatter x1, waiting for transfers between devices, on_device(): lax.psum_scatter(terms.astype(jnp.bfloat16), 'head', scatter_dimension=1,...  20.4 us
    all_to_all x1, blocking collectives, on_device(): lax.all_to_all(partial_sums.reshape(sources, rows_here, width + LANES), '...  13.5 us
    all_gather x1, blocking collectives, on_device(): table = lax.all_gather(page_table, 'req', axis=0, tiled=True)  10.9 us
    all_gather x1, blocking collectives, on_device(): lax.all_gather(queries.reshape(rows_here, width), 'req', axis=0, tiled=True)  10.5 us
    all_gather x1, blocking collectives, on_device(): lax.all_gather(attention.astype(jnp.bfloat16), 'req', axis=0, tiled=True)  8.9 us
    unnamed x1, blocking collectives  7.68 us
    reshape x1, local copies, waits for them, and re-layouts, on_device(): scale = scale.reshape(pages // GROUP, group_rows)  7.48 us
  transfers between devices with their start and end apart: 1, of which 1 were waited for; matrix products, arithmetic and copies ran while one was open for 0% of the time, Pallas kernels for 0%

profile of v1, /device:TPU:0, one launch (start us, length us, event | category | flops | bytes accessed | tf_op | source)
XLA Modules:
  0.0 156.7 jit_solution(17408326440663370600)
XLA Ops:
  6.5 0.0 reduce-scatter.2.cloned.1.call-start
  6.6 10.9 %all_gather.13 = s32[128,128]{1,0:T(8,128)S(1)} all-gather(s32[16,128]{1,0:T(8,128)} %param.14), channel_id=1, replica_groups=mesh['req'=8,'head'=4] {'req'}, dimensions={0}, use_global_device_ids=true | all-gather | bytes 73728 | tf_op jit(solution)/shard_map/all_gather | solution.py:168
  17.5 1.2 dynamic-slice
  19.4 0.9 dynamic-update-slice
  20.2 7.7 %all-reduce.lengths_ref = s32[128]{0:T(128)} all-reduce(s32[128]{0:T(128)S(1)} %dynamic-update-slice), channel_id=1, replica_groups=mesh['req'=8,'head'=4] {'req'}, use_global_device_ids=true, to_apply=%add | all-reduce | flops 128 | bytes 1024
  27.9 0.6 broadcast_subtract_fusion.table_ref
  28.5 4.6 %locate.1 = f32[32,96]{1,0:T(8,128)} custom-call(s32[128,128]{1,0:T(8,128)} %broadcast_subtract_fusion.table_ref, s32[128]{0:T(128)} %all-reduce.lengths_ref), custom_call_target="tpu_custom_call" | custom-call | tf_op jit(solution)/shard_map/locate/pallas_call | solution.py:175
  33.1 0.9 fusion.4
  34.0 0.1 lt.33
  34.1 0.2 compare_select_fusion
  34.3 5.9 %broadcast_in_dim.37 = f32[1024,16,2]{2,1,0:T(8,128)} broadcast(f32[1024,16]{1,0:T(8,128)S(1)} %compare_select_fusion), dimensions={0,1} | broadcast | bytes 196608 | tf_op jit(solution)/shard_map/broadcast_in_dim | solution.py:192
  40.2 0.0 copy-start.2
  40.2 7.5 %reshape.212.bias_ref = f32[128,256]{1,0:T(8,128)} reshape(f32[1024,16,2]{2,1,0:T(8,128)} %broadcast_in_dim.37) | data formatting | bytes 262144 | tf_op jit(solution)/shard_map/reshape | solution.py:193
  47.7 0.1 eq.24
  47.7 0.0 copy-done.2
  47.7 0.2 copy.11
  48.0 3.8 %broadcast_in_dim.20 = f32[1024,16,2]{2,1,0:T(8,128)} broadcast(f32[1024,2]{1,0:T(8,128)S(1)} %copy.11), dimensions={0,2} | broadcast | bytes 139264 | tf_op jit(solution)/shard_map/broadcast_in_dim | solution.py:194
  51.7 0.0 copy-start
  51.7 0.0 copy-start.1
  51.7 7.5 %reshape.211.scale_ref = f32[128,256]{1,0:T(8,128)} reshape(f32[1024,16,2]{2,1,0:T(8,128)} %broadcast_in_dim.20) | data formatting | bytes 262144 | tf_op jit(solution)/shard_map/reshape | solution.py:195
  59.2 0.0 copy-done
  59.2 10.5 %all_gather.12.q_ref = bf16[128,2048]{1,0:T(8,128)(2,1)} all-gather(bf16[16,2048]{1,0:T(8,128)(2,1)S(1)} %bitcast.15), channel_id=1, replica_groups=mesh['req'=8,'head'=4] {'req'}, dimensions={0}, use_global_device_ids=true | all-gather | bytes 589824 | tf_op jit(solution)/shard_map/all_gather | solution.py:170
  69.7 0.0 copy-done.1
  69.7 1.0 copy.12.vscale_ref
  70.8 1.0 compare_convert_fusion.member_ref
  71.8 0.8 and_select_fusion.block_ref
  72.6 29.9 %attend.1 = bf16[128,2176]{1,0:T(8,128)(2,1)} custom-call(bf16[128,2048]{1,0:T(8,128)(2,1)} %all_gather.12.q_ref, f32[1024,128]{1,0:T(8,128)} %compare_convert_fusion.member_ref, f32[128,256]{1,0:T(8,128)} %reshape.211.scale_ref, f32[128,256]{1,0:T(8,128)} %reshape.212.bias_ref, f32[128,256]{1,0:T(8,128)} %and_select_fusion.block_ref, ...), custom_call_target="tpu_custom_call" | custom-call | tf_op jit(solution)/shard_map/attend/pallas_call | solution.py:207
  102.4 13.5 %all_to_all.5 = bf16[8,16,2176]{2,1,0:T(8,128)(2,1)S(1)} all-to-all(bf16[8,16,2176]{2,1,0:T(8,128)(2,1)} %bitcast.14), channel_id=1, replica_groups=mesh['req'=8,'head'=4] {'req'}, dimensions={0} | all-to-all | bytes 1114112 | tf_op jit(solution)/shard_map/all_to_all | solution.py:226
  115.9 0.1 convert_element_type.29
  116.0 0.1 slice_reduce_fusion
  116.1 0.1 fusion.2
  116.2 0.1 fusion.3
  116.3 0.3 mul.27
  116.6 0.2 mul.28
  116.8 0.1 fusion
  116.9 8.9 %all_gather.15 = bf16[128,2048]{1,0:T(8,128)(2,1)S(1)} all-gather(bf16[16,2048]{1,0:T(8,128)(2,1)S(1)} %fusion), channel_id=1, replica_groups=mesh['req'=8,'head'=4] {'req'}, dimensions={0}, use_global_device_ids=true | all-gather | bytes 589824 | tf_op jit(solution)/shard_map/all_gather | solution.py:241
  125.8 3.6 %convolution_convert_fusion = bf16[128,1024]{1,0:T(8,128)(2,1)} fusion(bf16[128,2048]{1,0:T(8,128)(2,1)S(1)} %all_gather.15, bf16[2048,1024]{1,0:T(8,128)(2,1)} %param.15), kind=kOutput, calls=%fused_computation | convolution fusion | flops 537001984 | bytes 4980736 | tf_op jit(solution)/shard_map/dot_general | solution.py:240
  129.4 0.0 reduce-scatter.2.cloned.1.call-update
  129.5 20.4 %reduce-scatter.2.cloned.1.call-done = bf16[128,256]{1,0:T(8,128)(2,1)} async-done(((bf16[128,1024]{1,0:T(8,128)(2,1)}), bf16[128,256]{1,0:T(8,128)(2,1)}) %reduce-scatter.2.cloned.1.call-update) | async-done | bytes 65552 | tf_op jit(solution)/shard_map/reduce_scatter | solution.py:245
  (7 shorter events, 0.0 us)
Async XLA Ops:
  6.5 143.4 %reduce-scatter.2.cloned.1.call-start = ((), (), s32[]{:S(2)}) async-start(), calls=%async_computation.2 | async-start | bytes 327680 | tf_op jit(solution)/shard_map/reduce_scatter | solution.py:245
  40.2 7.5 %copy-start.2 = (f32[1024,2]{0,1:T(2,128)S(1)}, f32[1024,2]{0,1:T(2,128)}, u32[]{:S(2)}) copy-start(f32[1024,2]{0,1:T(2,128)} %param.11) | copy-start | bytes 24580
  51.7 7.5 %copy-start = (bf16[16,16,128]{2,1,0:T(8,128)(2,1)S(1)}, bf16[16,16,128]{2,1,0:T(8,128)(2,1)}, u32[]{:S(2)}) copy-start(bf16[16,16,128]{2,1,0:T(8,128)(2,1)} %param.8) | copy-start | bytes 196612
  51.7 18.0 %copy-start.1 = (f32[1024,2]{0,1:T(2,128)S(1)}, f32[1024,2]{0,1:T(2,128)}, u32[]{:S(2)}) copy-start(f32[1024,2]{0,1:T(2,128)} %param.12) | copy-start | bytes 24580
Sparse Core Ops, SparseCore 0:
  129.6 20.2 reduce-scatter.1

commit v2 on v1

v2 whole, which is shorter than its diff:
```python
import functools
import math

import jax
import jax.numpy as jnp
from jax import lax
from jax.experimental import pallas as pl
from jax.experimental.pallas import tpu as pltpu
from jax.sharding import PartitionSpec as P

floor_score = -1e30
GROUP = 8
LANES = 128


def greet(peers):
    barrier = pltpu.get_barrier_semaphore()
    for peer in peers:
        pl.semaphore_signal(
            barrier, inc=1, device_id=peer, device_id_type=pl.DeviceIdType.MESH
        )
    pl.semaphore_wait(barrier, len(peers))


def send(src, dst, send_sem, recv_sem, peer):
    copy = pltpu.make_async_remote_copy(
        src_ref=src,
        dst_ref=dst,
        send_sem=send_sem,
        recv_sem=recv_sem,
        device_id=peer,
        device_id_type=pl.DeviceIdType.MESH,
    )
    copy.start()
    return copy


def gather_kernel(
    sources, base, code_ref, q_ref, found_ref, q_all, codes, acc, q_send, q_recv, c_send, c_recv
):
    me, z = lax.axis_index("req"), lax.axis_index("head")
    rows, width = code_ref.shape
    requests = codes.shape[0]
    high_rows = found_ref.shape[0]
    peers = [(lax.rem(me + d, sources), z) for d in range(1, sources)]
    greet(peers)
    mine = pl.ds(pl.multiple_of(me * rows, rows), rows)
    code_copies = [
        send(code_ref, codes.at[mine], c_send.at[i], c_recv.at[i], peer)
        for i, peer in enumerate(peers)
    ]
    q_copies = [
        send(q_ref, q_all.at[mine], q_send.at[i], q_recv.at[i], peer)
        for i, peer in enumerate(peers)
    ]
    codes[mine, :] = code_ref[...]
    q_all[mine, :] = q_ref[...]
    for copy in code_copies:
        copy.wait()

    acc[...] = jnp.zeros_like(acc)
    iota_hi = lax.broadcasted_iota(jnp.int32, (high_rows, width), 0)
    iota_lo = lax.broadcasted_iota(jnp.int32, (GROUP, width), 0)
    offset = me * (high_rows * GROUP)
    step = 8

    def body(i, carry):
        lefts, rights = [], []
        block = codes[pl.ds(pl.multiple_of(i * step, step), step), :]
        page = (block >> base) - offset
        live_all = (block & ((1 << base) - 1)).astype(jnp.float32)
        for t in range(step):
            r = i * step + t
            row = page[t : t + 1, :]
            lefts.append(jnp.where(iota_hi == (row >> 3), 1.0, 0.0).astype(jnp.bfloat16))
            same = iota_lo == (row & (GROUP - 1))
            parts = [
                jnp.where(same, (r // 256).astype(jnp.float32), 0.0),
                jnp.where(same, (r % 256).astype(jnp.float32), 0.0),
                jnp.where(same, live_all[t : t + 1, :], 0.0),
                jnp.zeros(same.shape, jnp.float32),
            ]
            rights.append(jnp.concatenate(parts, axis=0).astype(jnp.bfloat16))
        acc[...] += lax.dot_general(
            jnp.concatenate(lefts, axis=1),
            jnp.concatenate(rights, axis=1),
            (((1,), (1,)), ((), ())),
            preferred_element_type=jnp.float32,
        )
        return carry

    lax.fori_loop(0, requests // step, body, 0)
    found_ref[...] = acc[...]
    for copy in q_copies:
        copy.wait()


def project_kernel(
    sources,
    parts,
    heads,
    sums_ref,
    weight_ref,
    out_ref,
    weight,
    got,
    own,
    rows_all,
    terms,
    terms_in,
    w_sem,
    s_send,
    s_recv,
    a_send,
    a_recv,
    t_send,
    t_recv,
):
    me, z = lax.axis_index("req"), lax.axis_index("head")
    rows = own.shape[0]
    dim = LANES
    load = pltpu.make_async_copy(weight_ref, weight, w_sem)
    load.start()
    peers = [(lax.rem(me + d, sources), z) for d in range(1, sources)]
    others = [(me, lax.rem(z + d, parts)) for d in range(1, parts)]
    greet(peers + others)
    copies = []
    for i, peer in enumerate(peers):
        theirs = pl.ds(pl.multiple_of(peer[0] * rows, rows), rows)
        copies.append(send(sums_ref.at[theirs], got.at[me], s_send.at[i], s_recv.at[i], peer))
    mine = pl.ds(pl.multiple_of(me * rows, rows), rows)
    got[me] = sums_ref[mine, :]
    for copy in copies:
        copy.wait()

    tails = [got[i, :, heads * dim :].astype(jnp.float32) for i in range(sources)]
    peaks = [t[:, 2 * heads : 3 * heads] for t in tails]
    top = functools.reduce(jnp.maximum, peaks)
    factors = [jnp.exp(p - top) for p in peaks]
    dens = [t[:, :heads] + t[:, heads : 2 * heads] for t in tails]
    total = functools.reduce(jnp.add, [f * d for f, d in zip(factors, dens)])
    factors = [f / total for f in factors]
    for h in range(heads):
        cols = slice(h * dim, (h + 1) * dim)
        value = jnp.zeros((rows, dim), jnp.float32)
        for i in range(sources):
            value += got[i, :, cols].astype(jnp.float32) * factors[i][:, h : h + 1]
        own[:, cols] = value.astype(jnp.bfloat16)
    copies = [
        send(own, rows_all.at[mine], a_send.at[i], a_recv.at[i], peer)
        for i, peer in enumerate(peers)
    ]
    rows_all[mine, :] = own[...]
    load.wait()
    for copy in copies:
        copy.wait()

    width = out_ref.shape[1]

    def product(part):
        cols = pl.ds(pl.multiple_of(part * width, width), width)
        return jnp.dot(rows_all[...], weight[:, cols], preferred_element_type=jnp.float32)

    aligned = width % LANES == 0
    if not aligned:
        full = jnp.dot(rows_all[...], weight[...], preferred_element_type=jnp.float32)
        for part in range(parts):
            terms[part] = full[:, part * width : (part + 1) * width].astype(jnp.bfloat16)
    copies = []
    for i, peer in enumerate(others):
        part = peer[1]
        if aligned:
            terms[part] = product(part).astype(jnp.bfloat16)
        copies.append(send(terms.at[part], terms_in.at[i], t_send.at[i], t_recv.at[i], peer))
    result = product(z) if aligned else terms[z].astype(jnp.float32)
    for i, copy in enumerate(copies):
        copy.wait()
        result += terms_in[i].astype(jnp.float32)
    out_ref[...] = result.astype(jnp.bfloat16)


def attend_kernel(
    kv_local,
    page_size,
    q_ref,
    found_ref,
    kscale_ref,
    vscale_ref,
    k_ref,
    v_ref,
    out_ref,
    member_ref,
    bias_ref,
    block_ref,
    scales,
    q_rows,
    m_rows,
    sums,
    shift,
    extra,
):
    heads, pages, dim = q_rows.shape
    requests = q_ref.shape[0]
    group_rows = bias_ref.shape[1]
    per_head = heads // kv_local
    steps = pl.num_programs(0)
    pid = pl.program_id(0)
    groups = k_ref.shape[0] // group_rows

    @pl.when(pid == 0)
    def _():
        found = found_ref[...].astype(jnp.bfloat16)
        page_rows = page_size * kv_local
        iota = lambda shape, axis: lax.broadcasted_iota(jnp.int32, shape, axis)
        spread_shape = (found.shape[1], group_rows)
        spread = iota(spread_shape, 0) - 2 * GROUP == iota(spread_shape, 1) // page_rows
        spread = jnp.where(spread, 1.0, 0.0).astype(jnp.bfloat16)
        live = jnp.dot(found, spread, preferred_element_type=jnp.float32)
        token = (iota(live.shape, 1) % page_rows) // kv_local
        bias_ref[...] = jnp.where(token.astype(jnp.float32) < live, 0.0, floor_score)
        row, col = iota(block_ref.shape, 0), iota(block_ref.shape, 1)
        same = (row % GROUP == col // page_rows) & (row // GROUP // per_head == col % kv_local)
        block_ref[...] = jnp.where(same, 0.0, floor_score)
        repeat_shape = (pages, found.shape[0])
        repeat = iota(repeat_shape, 0) // GROUP == iota(repeat_shape, 1)
        repeat = jnp.where(repeat, 1.0, 0.0).astype(jnp.bfloat16)
        rows = jnp.dot(repeat, found, preferred_element_type=jnp.float32)
        lane, slot = iota(rows.shape, 1), iota(rows.shape, 0) % GROUP
        digit = jnp.where(lane == slot, 256.0, jnp.where(lane == slot + GROUP, 1.0, 0.0))
        owner = jnp.sum(rows * digit, axis=1, keepdims=True)
        ids = iota(member_ref.shape, 1).astype(jnp.float32)
        member_ref[...] = jnp.where(owner == ids, 1.0, 0.0)
        member = member_ref[...].astype(jnp.bfloat16)
        root = 1.0 / math.sqrt(dim)
        spare = jnp.zeros((8 - 2 * kv_local, pages), jnp.float32)
        stacked = jnp.concatenate([kscale_ref[...] * root, vscale_ref[...], spare], axis=0)
        scales[...] = stacked.T

        def pick(i, carry):
            cols = q_ref[:, pl.ds(pl.multiple_of(i * 2 * dim, 2 * dim), 2 * dim)]
            got = jnp.dot(member, cols, preferred_element_type=jnp.float32)
            q_rows[2 * i] = got[:, :dim]
            q_rows[2 * i + 1] = got[:, dim:]
            return carry

        lax.fori_loop(0, heads // 2, pick, 0)

    def group(i, carry):
        g = pid * groups + i
        p0 = pl.multiple_of(g * GROUP, GROUP)
        q = jnp.concatenate([q_rows[h, pl.ds(p0, GROUP), :] for h in range(heads)], axis=0)
        start = pl.multiple_of(i * group_rows, group_rows)
        kk = k_ref[pl.ds(start, group_rows), :]
        vv = v_ref[pl.ds(start, group_rows), :]
        s = lax.dot_general(
            q.astype(jnp.bfloat16), kk, (((1,), (1,)), ((), ())), preferred_element_type=jnp.float32
        )
        factors = [scales[pl.ds(p0, GROUP), k : k + 1] for k in range(2 * kv_local)]
        row_scale = jnp.concatenate([factors[h // per_head] for h in range(heads)], axis=0)
        s = (s * row_scale + bias_ref[pl.ds(g, 1), :]) + block_ref[...]
        top = jnp.max(s, axis=1, keepdims=True)
        w = jnp.exp(s - top).astype(jnp.bfloat16)
        both = jnp.concatenate([vv, jnp.ones_like(vv)], axis=1)
        o = jnp.dot(w, both, preferred_element_type=jnp.float32)
        for h in range(heads):
            rows = slice(h * GROUP, (h + 1) * GROUP)
            sums[h, pl.ds(p0, GROUP), :dim] = o[rows, :dim] * factors[kv_local + h // per_head]
            sums[h, pl.ds(p0, GROUP), dim:] = o[rows, dim:]
            m_rows[h, pl.ds(p0, GROUP), :] = jnp.broadcast_to(top[rows], (GROUP, dim))
        return carry

    lax.fori_loop(0, groups, group, 0, unroll=4)

    @pl.when(pid == steps - 1)
    def _():
        shift[...] = jnp.zeros_like(shift)
        extra[...] = jnp.zeros_like(extra)
        lane = lax.broadcasted_iota(jnp.int32, extra.shape, 1)

        def finish(h, carry):
            inside = member_ref[...] > 0.5
            top = jnp.concatenate([m_rows[h]] * (requests // dim), axis=1)
            peak = jnp.max(jnp.where(inside, top, floor_score), axis=0, keepdims=True)
            peak = peak.astype(jnp.bfloat16).astype(jnp.float32)
            f = jnp.where(inside, jnp.exp(top - peak), 0.0).astype(jnp.bfloat16)
            got = lax.dot_general(
                f,
                sums[h].astype(jnp.bfloat16),
                (((0,), (0,)), ((), ())),
                preferred_element_type=jnp.float32,
            )
            cols = pl.ds(pl.multiple_of(h * dim, dim), dim)
            out_ref[:, cols] = got[:, :dim].astype(jnp.bfloat16)
            den = got[:, dim:]
            den_high = den.astype(jnp.bfloat16).astype(jnp.float32)
            kept = jnp.where(lane == h, den_high, extra[...])
            extra[...] = jnp.where(lane == heads + h, den - den_high, kept)
            shift[pl.ds(2 * heads + h, 1), :] = peak
            return carry

        lax.fori_loop(0, heads, finish, 0)
        tail = jnp.where(lane < 2 * heads, extra[...], shift[...].T)
        out_ref[:, heads * dim :] = tail.astype(jnp.bfloat16)


def on_device(
    queries,
    k_codes,
    value_quantized_codes,
    key_page_scale,
    value_page_scale,
    lengths,
    page_table,
    out_weight,
):
    pages, page_size, kv_local, dim = k_codes.shape
    rows_here, heads, _ = queries.shape
    width = heads * dim
    vmem = pl.BlockSpec(memory_space=pltpu.VMEM)
    sources, parts = lax.axis_size("req"), lax.axis_size("head")
    requests = sources * rows_here
    table_width = page_table.shape[1]
    base = page_size.bit_length()
    entry = jnp.arange(table_width, dtype=jnp.int32)[None, :] * page_size
    live = jnp.clip(lengths[:, None] - entry, 0, page_size)
    code = jnp.where(live > 0, page_table * (1 << base) + live, -1)

    dma = pltpu.SemaphoreType.DMA
    groups = pages // GROUP
    found, q_all = pl.pallas_call(
        functools.partial(gather_kernel, sources, base),
        out_shape=[
            jax.ShapeDtypeStruct((groups, 4 * GROUP), jnp.float32),
            jax.ShapeDtypeStruct((requests, width), jnp.bfloat16),
        ],
        in_specs=[vmem, vmem],
        out_specs=[vmem, vmem],
        scratch_shapes=[
            pltpu.VMEM((requests, table_width), jnp.int32),
            pltpu.VMEM((groups, 4 * GROUP), jnp.float32),
        ]
        + [dma((sources - 1,))] * 4,
        compiler_params=pltpu.CompilerParams(collective_id=0, has_side_effects=True),
        name="gather",
    )(code, queries.reshape(rows_here, width))

    page_rows = page_size * kv_local
    group_rows = GROUP * page_rows
    k_rows = k_codes.reshape(pages * page_rows, dim)
    v_rows = value_quantized_codes.reshape(pages * page_rows, dim)
    block_pages = 128
    steps = pages // block_pages
    whole = lambda shape: pl.BlockSpec(shape, lambda i: (0,) * len(shape))
    stream = pl.BlockSpec((block_pages * page_rows, dim), lambda i: (i, 0))
    partial_sums = pl.pallas_call(
        functools.partial(attend_kernel, kv_local, page_size),
        grid=(steps,),
        out_shape=jax.ShapeDtypeStruct((requests, width + LANES), jnp.bfloat16),
        in_specs=[vmem, vmem, vmem, vmem, stream, stream],
        out_specs=whole((requests, width + LANES)),
        scratch_shapes=[
            pltpu.VMEM((pages, requests), jnp.float32),
            pltpu.VMEM((groups, group_rows), jnp.float32),
            pltpu.VMEM((heads * GROUP, group_rows), jnp.float32),
            pltpu.VMEM((pages, 8), jnp.float32),
            pltpu.VMEM((heads, pages, dim), jnp.float32),
            pltpu.VMEM((heads, pages, dim), jnp.float32),
            pltpu.VMEM((heads, pages, 2 * dim), jnp.float32),
            pltpu.VMEM((LANES, requests), jnp.float32),
            pltpu.VMEM((requests, LANES), jnp.float32),
        ],
        compiler_params=pltpu.CompilerParams(
            vmem_limit_bytes=60 * 1024 * 1024, dimension_semantics=("arbitrary",)
        ),
        name="attend",
    )(q_all, found, key_page_scale.T, value_page_scale.T, k_rows, v_rows)

    columns = out_weight.shape[1] // parts
    return pl.pallas_call(
        functools.partial(project_kernel, sources, parts, heads),
        out_shape=jax.ShapeDtypeStruct((requests, columns), jnp.bfloat16),
        in_specs=[vmem, pl.BlockSpec(memory_space=pl.ANY)],
        out_specs=vmem,
        scratch_shapes=[
            pltpu.VMEM(out_weight.shape, jnp.bfloat16),
            pltpu.VMEM((sources, rows_here, width + LANES), jnp.bfloat16),
            pltpu.VMEM((rows_here, width), jnp.bfloat16),
            pltpu.VMEM((requests, width), jnp.bfloat16),
            pltpu.VMEM((parts, requests, columns), jnp.bfloat16),
            pltpu.VMEM((parts - 1, requests, columns), jnp.bfloat16),
            dma,
        ]
        + [dma((sources - 1,))] * 4
        + [dma((parts - 1,))] * 2,
        compiler_params=pltpu.CompilerParams(
            collective_id=1, has_side_effects=True, vmem_limit_bytes=40 * 1024 * 1024
        ),
        name="project",
    )(partial_sums, out_weight)


def solution(mesh):
    in_specs = (
        P("req", "head", None),
        P("req", None, "head", None),
        P("req", None, "head", None),
        P("req", "head"),
        P("req", "head"),
        P("req"),
        P("req", None),
        P("head", "req"),
    )
    out_specs = P(None, ("req", "head"))
    return jax.shard_map(
        on_device, mesh=mesh, in_specs=in_specs, out_specs=out_specs, check_vma=False
    )
```

time: 157 us -> 79.5 us (0.51)
  blocking collectives: 51.5 us -> 0 us
  Pallas kernels: 34.4 us -> 72.2 us
  local copies, waits for them, and re-layouts: 28.6 us -> 5.36 us
  waiting for transfers between devices: 20.4 us -> 0 us
  between operations: 14.2 us -> 0.02 us
  matrix products: 3.64 us -> 0 us
  other arithmetic: 3.99 us -> 1.37 us
    pallas_call x2 -> x3, Pallas kernels: 34.4 us -> 72.2 us  [the longest x1 32.2 us: on_device(): pl.pallas_call(functools.partial(attend_kernel, kv_local, page_size), gri...]
    all_gather x3 -> x0, blocking collectives: 30.3 us -> none  [the longest x1 10.9 us: on_device(): table = lax.all_gather(page_table, 'req', axis=0, tiled=True)]
    reduce_scatter x1 -> x0, waiting for transfers between devices: 20.4 us -> none  [on_device(): lax.psum_scatter(terms.astype(jnp.bfloat16), 'head', scatter_dimension=1,...]
    reshape x2 -> x0, local copies, waits for them, and re-layouts: 14.9 us -> none  [the longest x1 7.48 us: on_device(): scale = scale.reshape(pages // GROUP, group_rows)]
    all_to_all x1 -> x0, blocking collectives: 13.5 us -> none  [on_device(): lax.all_to_all(partial_sums.reshape(sources, rows_here, width + LANES), '...]
    broadcast_in_dim x2 -> x0, local copies, waits for them, and re-layouts: 9.65 us -> none  [the longest x1 5.89 us: on_device(): jnp.broadcast_to(token < live[:, None, None], full)]
    unnamed x1 -> x0, blocking collectives: 7.68 us -> none
    dot_general x1 -> x0, matrix products: 3.64 us -> none  [on_device(): jnp.dot(lax.all_gather(attention.astype(jnp.bfloat16), 'req', axis=0, til...]
  transfers between devices with their start and end apart: 1 -> 0, of which waited for: 1 -> 0; matrix products, arithmetic and copies ran while one was open for 0% -> 0% of each run, Pallas kernels for 0% -> 0%
where the time goes in v2:
time: 79.5 us; the launch traced here: 79 us
  Pallas kernels  72.2 us (91%)
  local copies, waits for them, and re-layouts  5.36 us (7%)
  other arithmetic  1.37 us (2%)
    pallas_call x1, Pallas kernels, on_device(): pl.pallas_call(functools.partial(attend_kernel, kv_local, page_size), gri...  32.2 us
    pallas_call x1, Pallas kernels, on_device(): pl.pallas_call(functools.partial(project_kernel, sources, parts, heads),...  27.2 us
    pallas_call x1, Pallas kernels, on_device(): pl.pallas_call(functools.partial(gather_kernel, sources, base), out_shape...  12.9 us
    unnamed x6, local copies, waits for them, and re-layouts  5.36 us

profile of v2, /device:TPU:0, one launch (start us, length us, event | category | flops | bytes accessed | tf_op | source)
XLA Modules:
  0.0 79.0 jit_solution(2530701521097263582)
XLA Ops:
  0.0 1.4 %add_select_fusion.code_ref = s32[16,128]{1,0:T(8,128)} fusion(s32[16,128]{1,0:T(8,128)} %param.14, s32[128]{0:T(128)S(1)} %iota_multiply_fusion, s32[16]{0:T(128)} %param.13), kind=kLoop, calls=%fused_computation.1 | loop fusion | flops 12288 | bytes 16960 | tf_op jit(solution)/shard_map/jit(_where)/select_n | solution.py:326
  1.4 1.5 %copy.11 = bf16[2,8,16,128]{3,1,2,0:T(8,128)(2,1)} copy(bf16[2,8,16,128]{3,2,1,0:T(8,128)(2,1)} %bitcast.11) | data formatting | bytes 131072
  2.9 12.9 %gather.1 = (f32[128,32]{1,0:T(8,128)}, bf16[128,2048]{1,0:T(8,128)(2,1)}) custom-call(s32[16,128]{1,0:T(8,128)} %add_select_fusion.code_ref, bf16[16,2048]{1,0:T(8,128)(2,1)} %bitcast.10), custom_call_target="tpu_custom_call" | custom-call | tf_op jit(solution)/shard_map/gather/pallas_call | solution.py:330
  15.7 32.2 %attend.1.sums_ref = bf16[128,2176]{1,0:T(8,128)(2,1)} custom-call(bf16[128,2048]{1,0:T(8,128)(2,1)} %get-tuple-element.7.q_ref, f32[128,32]{1,0:T(8,128)} %get-tuple-element.8.found_ref, f32[2,1024]{1,0:T(2,128)} %bitcast.12, f32[2,1024]{1,0:T(2,128)} %bitcast.13, bf16[32768,128]{1,0:T(8,128)(2,1)} %bitcast.8, bf16[32768,128]{1,0:T(8,128)(2,1)} %bitcast.9), custom_call_target="tpu_custom_call" | custom-call | tf_op jit(solution)/shard_map/attend/pallas_call | solution.py:355
  47.9 0.0 copy-start
  47.9 2.2 %copy-done = bf16[2048,1024]{1,0:T(8,128)(2,1)S(1)} copy-done((bf16[2048,1024]{1,0:T(8,128)(2,1)S(1)}, bf16[2048,1024]{1,0:T(8,128)(2,1)}, u32[]{:S(2)}) %copy-start) | copy-done | bytes 4194328
  50.1 0.0 copy-start.1
  50.1 1.1 %copy-done.1 = bf16[128,2176]{1,0:T(8,128)(2,1)S(1)} copy-done((bf16[128,2176]{1,0:T(8,128)(2,1)S(1)}, bf16[128,2176]{1,0:T(8,128)(2,1)}, u32[]{:S(2)}) %copy-start.1) | copy-done | bytes 557080
  51.1 27.2 %project.1 = bf16[128,256]{1,0:T(8,128)(2,1)S(1)} custom-call(bf16[128,2176]{1,0:T(8,128)(2,1)S(1)} %copy-done.1, bf16[2048,1024]{1,0:T(8,128)(2,1)S(1)} %copy-done), custom_call_target="tpu_custom_call" | custom-call | tf_op jit(solution)/shard_map/project/pallas_call | solution.py:379
  78.3 0.6 copy.13
  (1 shorter events, 0.0 us)
Async XLA Ops:
  47.9 2.2 %copy-start = (bf16[2048,1024]{1,0:T(8,128)(2,1)S(1)}, bf16[2048,1024]{1,0:T(8,128)(2,1)}, u32[]{:S(2)}) copy-start(bf16[2048,1024]{1,0:T(8,128)(2,1)} %weight_ref.1) | copy-start | bytes 12582916
  50.1 1.1 %copy-start.1 = (bf16[128,2176]{1,0:T(8,128)(2,1)S(1)}, bf16[128,2176]{1,0:T(8,128)(2,1)}, u32[]{:S(2)}) copy-start(bf16[128,2176]{1,0:T(8,128)(2,1)} %attend.1.sums_ref) | copy-start | bytes 1671172

commit v3 on v2

--- a/solution.py
+++ b/solution.py
@@ -89,7 +89,7 @@
         )
         return carry
 
-    lax.fori_loop(0, requests // step, body, 0)
+    lax.fori_loop(0, requests // step, body, 0, unroll=2)
     found_ref[...] = acc[...]
     for copy in q_copies:
         copy.wait()
@@ -269,7 +269,7 @@
             m_rows[h, pl.ds(p0, GROUP), :] = jnp.broadcast_to(top[rows], (GROUP, dim))
         return carry
 
-    lax.fori_loop(0, groups, group, 0, unroll=4)
+    lax.fori_loop(0, groups, group, 0, unroll=8)
 
     @pl.when(pid == steps - 1)
     def _():
@@ -298,7 +298,7 @@
             shift[pl.ds(2 * heads + h, 1), :] = peak
             return carry
 
-        lax.fori_loop(0, heads, finish, 0)
+        lax.fori_loop(0, heads, finish, 0, unroll=4)
         tail = jnp.where(lane < 2 * heads, extra[...], shift[...].T)
         out_ref[:, heads * dim :] = tail.astype(jnp.bfloat16)
 
@@ -393,7 +393,7 @@
         + [dma((sources - 1,))] * 4
         + [dma((parts - 1,))] * 2,
         compiler_params=pltpu.CompilerParams(
-            collective_id=1, has_side_effects=True, vmem_limit_bytes=40 * 1024 * 1024
+            collective_id=1, has_side_effects=True, vmem_limit_bytes=63 * 1024 * 1024
         ),
         name="project",
     )(partial_sums, out_weight)

time: 79.5 us -> 67.2 us (0.85)
  Pallas kernels: 72.2 us -> 62.3 us
  local copies, waits for them, and re-layouts: 5.36 us -> 2.96 us
    pallas_call x1, Pallas kernels: 32.2 us -> 21.4 us  [on_device(): pl.pallas_call(functools.partial(attend_kernel, kv_local, page_size), gri...]
    unnamed x6 -> x2, local copies, waits for them, and re-layouts: 5.36 us -> 2.96 us
    pallas_call x1, Pallas kernels: 27.2 us -> 28 us  [on_device(): pl.pallas_call(functools.partial(project_kernel, sources, parts, heads),...]
where the time goes in v3:
time: 67.2 us; the launch traced here: 66.6 us
  Pallas kernels  62.3 us (93%)
  local copies, waits for them, and re-layouts  2.96 us (4%)
  other arithmetic  1.36 us (2%)
    pallas_call x1, Pallas kernels, on_device(): pl.pallas_call(functools.partial(project_kernel, sources, parts, heads),...  28 us
    pallas_call x1, Pallas kernels, on_device(): pl.pallas_call(functools.partial(attend_kernel, kv_local, page_size), gri...  21.4 us
    pallas_call x1, Pallas kernels, on_device(): pl.pallas_call(functools.partial(gather_kernel, sources, base), out_shape...  12.9 us
    unnamed x2, local copies, waits for them, and re-layouts  2.96 us
    select_n x1, other arithmetic, on_device(): code = jnp.where(live > 0, page_table * (1 << base) + live, -1)  1.36 us

profile of v3, /device:TPU:0, one launch (start us, length us, event | category | flops | bytes accessed | tf_op | source)
XLA Modules:
  0.0 66.6 jit_solution(10418396300611462797)
XLA Ops:
  0.0 1.4 %add_select_fusion.code_ref = s32[16,128]{1,0:T(8,128)} fusion(s32[16,128]{1,0:T(8,128)} %param.14, s32[128]{0:T(128)S(1)} %iota_multiply_fusion, s32[16]{0:T(128)} %param.13), kind=kLoop, calls=%fused_computation.1 | loop fusion | flops 12288 | bytes 16960 | tf_op jit(solution)/shard_map/jit(_where)/select_n | solution.py:326
  1.4 1.5 %copy.11 = bf16[2,8,16,128]{3,1,2,0:T(8,128)(2,1)} copy(bf16[2,8,16,128]{3,2,1,0:T(8,128)(2,1)} %bitcast.11) | data formatting | bytes 131072
  2.9 12.9 %gather.1 = (f32[128,32]{1,0:T(8,128)}, bf16[128,2048]{1,0:T(8,128)(2,1)}) custom-call(s32[16,128]{1,0:T(8,128)} %add_select_fusion.code_ref, bf16[16,2048]{1,0:T(8,128)(2,1)} %bitcast.10), custom_call_target="tpu_custom_call" | custom-call | tf_op jit(solution)/shard_map/gather/pallas_call | solution.py:330
  15.7 21.4 %attend.1.sums_ref = bf16[128,2176]{1,0:T(8,128)(2,1)} custom-call(bf16[128,2048]{1,0:T(8,128)(2,1)} %get-tuple-element.7.q_ref, f32[128,32]{1,0:T(8,128)} %get-tuple-element.8.found_ref, f32[2,1024]{1,0:T(2,128)} %bitcast.12, f32[2,1024]{1,0:T(2,128)} %bitcast.13, bf16[32768,128]{1,0:T(8,128)(2,1)} %bitcast.8, bf16[32768,128]{1,0:T(8,128)(2,1)} %bitcast.9), custom_call_target="tpu_custom_call" | custom-call | tf_op jit(solution)/shard_map/attend/pallas_call | solution.py:355
  37.1 28.0 %project.1 = bf16[128,256]{1,0:T(8,128)(2,1)} custom-call(bf16[128,2176]{1,0:T(8,128)(2,1)} %attend.1.sums_ref, bf16[2048,1024]{1,0:T(8,128)(2,1)} %weight_ref.1), custom_call_target="tpu_custom_call" | custom-call | tf_op jit(solution)/shard_map/project/pallas_call | solution.py:379
  65.1 1.5 %copy.13 = bf16[128,256]{1,0:T(8,128)(2,1)} copy(bf16[128,256]{1,0:T(8,128)(2,1)} %project.1) | data formatting | bytes 131072
  (1 shorter events, 0.0 us)
